TPU v7x, 32 devices: a whole 2x2x4 slice. The times are simulated.
32 devices in a mesh: grp: 2 (over y), seq: 16 (over z, x, core).
Axes of the slice: x: 2, y: 2, z: 4, core: 2. Of those that a mesh axis runs over, the one named last changes fastest.
Arguments:
- frames: bfloat16 [4, 10240, 1280], P('grp', 'seq'), parts along dimension 0, may hold values from -120 to 120
- dec_states: bfloat16 [2, 256, 1280], P(None, 'grp'), parts along dimension 1, may hold values from -6 to 6
- w_query: bfloat16 [1280, 1280], P(None, 'seq'), may hold values from -0.15625 to 0.15625
- w_keyval: bfloat16 [1280, 2560], replicated, may hold values from -0.15625 to 0.15625
- w_output: bfloat16 [1280, 1280], P(None, 'seq'), may hold values from -0.15625 to 0.15625
- head_slope: float32 [20], replicated, may hold values from 0.3 to 12
- lengths: int32 [4, 16], P('grp'), parts along dimension 0, may hold values from 128 to 640, as said below
- positions: int32 [2, 256], P(None, 'grp'), parts along dimension 1, may hold values from 0 to 15
Outputs:
- attended: bfloat16 [2, 256, 1280], P(None, 'grp', 'seq'), parts along dimension 1
There are 2 independent parts, one for each index of `grp`. A program takes and returns all parts, laid end to end along the dimension named above; an argument that names none is the same for every part. Nothing has to cross between parts.
Inputs may be any that keep to these rules, and one draw needn't show every extreme that they name: `lengths`: every step has one block of exactly 640 valid frames.
All inputs are finite; a program needn't handle non-finite values.
Results may differ from a plain program's by a relative error of at most 0.005.
The roundings to bfloat16 on the way count: a program that leaves them out, or rounds other values in their place, can miss the bound.
Values may be sent and summed in bfloat16 or wider, within the bound.
A program may use at most 128 MiB of HBM per device.

v0:
```python
import functools
import math
import jax
import jax.numpy as jnp
from jax import lax
from jax.sharding import PartitionSpec as P


def block_partial(
    queries,
    block_keys,
    block_values,
    length_now,
    slot_place,
    age_steps,
    row_positions,
    head_slope,
    devices,
):
    query_rows, head_count, head_size = queries.shape
    frame_count = block_keys.shape[0]
    keys_split = block_keys.reshape(frame_count, head_count, head_size)
    scores = jnp.einsum(
        "qhd,jhd->hqj", queries, keys_split, preferred_element_type=jnp.float32
    ) / math.sqrt(head_size)
    distance = (
        jnp.abs(row_positions.astype(jnp.float32) - slot_place.astype(jnp.float32)) / devices
        + age_steps
    )
    scores = scores - head_slope[:, None, None] * distance[None, :, None]
    valid = lax.broadcasted_iota(jnp.int32, (1, 1, frame_count), 2) < length_now
    scores = jnp.where(valid, scores, -jnp.inf)
    row_peak = jnp.max(scores, axis=2)
    weights = jnp.exp(scores - row_peak[:, :, None]).astype(jnp.bfloat16)
    row_total = jnp.sum(weights.astype(jnp.float32), axis=2)
    values_split = block_values.reshape(frame_count, head_count, head_size)
    row_context = jnp.einsum(
        "hqj,jhd->qhd", weights, values_split, preferred_element_type=jnp.float32
    )
    return (row_peak.T, row_total.T, row_context.reshape(query_rows, head_count * head_size))


def rescale(row_context, factors, head_count):
    query_rows = row_context.shape[0]
    spread_rows = row_context.reshape(query_rows, head_count, -1) * factors[:, :, None]
    return spread_rows.reshape(query_rows, -1)


def combine_parts(head_count, earlier, later):
    peak_one, total_one, context_one = earlier
    peak_two, total_two, context_two = later
    row_top = jnp.maximum(peak_one, peak_two)
    scale_one = jnp.exp(peak_one - row_top)
    scale_two = jnp.exp(peak_two - row_top)
    merged_total = total_one * scale_one + total_two * scale_two
    merged_context = rescale(context_one, scale_one, head_count) + rescale(
        context_two, scale_two, head_count
    )
    return (row_top, merged_total, merged_context)


def local(frames, dec_states, w_query, w_keyval, w_output, head_slope, lengths, positions):
    devices = lax.axis_size("seq")
    own_index = lax.axis_index("seq")
    step_count, frame_count, model_width = frames.shape
    query_rows = dec_states.shape[1]
    head_count = head_slope.shape[0]
    head_size = model_width // head_count
    frame_rows = frames.reshape(step_count * frame_count, model_width)
    keyval = jnp.dot(frame_rows, w_keyval, preferred_element_type=jnp.float32).astype(jnp.bfloat16)
    block_keys = keyval[:, :model_width].reshape(step_count, frame_count, model_width)
    block_values = keyval[:, model_width:].reshape(step_count, frame_count, model_width)
    dec_rows = dec_states.reshape(step_count * query_rows, model_width)
    local_query = jnp.dot(dec_rows, w_query, preferred_element_type=jnp.float32).astype(
        jnp.bfloat16
    )
    queries = lax.all_gather(local_query, "seq", axis=1, tiled=True)
    queries = queries.reshape(step_count, query_rows, head_count, head_size)
    combine = functools.partial(combine_parts, head_count)
    slot_place = (own_index + 1) % devices
    results = []
    for step_now in range(step_count):
        running = None
        for older_step in range(step_now + 1):
            partial_now = block_partial(
                queries[step_now],
                block_keys[older_step],
                block_values[older_step],
                lengths[older_step, own_index],
                slot_place,
                float(step_now - older_step),
                positions[step_now],
                head_slope,
                devices,
            )
            running = partial_now if running is None else combine(running, partial_now)
        row_peak, row_total, row_context = running
        row_top = lax.pmax(row_peak, "seq")
        factors = jnp.exp(row_peak - row_top)
        row_total, row_context = lax.psum(
            (row_total * factors, rescale(row_context, factors, head_count)), "seq"
        )
        context = row_context.reshape(query_rows, head_count, head_size) / row_total[:, :, None]
        context = context.reshape(query_rows, model_width).astype(jnp.bfloat16)
        results.append(
            jnp.dot(context, w_output, preferred_element_type=jnp.float32).astype(jnp.bfloat16)
        )
    return jnp.stack(results)


def solution(mesh):
    return jax.shard_map(
        local,
        mesh=mesh,
        in_specs=(
            P("grp", "seq", None),
            P(None, "grp", None),
            P(None, "seq"),
            P(),
            P(None, "seq"),
            P(),
            P("grp", None),
            P(None, "grp"),
        ),
        out_specs=P(None, "grp", "seq"),
        check_vma=False,
    )
```

profile of v0, /device:TPU:0, one launch (start us, length us, event | category | flops | bytes accessed | tf_op | source)
XLA Modules:
  0.0 259.9 jit_solution(2014881977530584230)
XLA Ops:
  6.5 0.0 copy-start
  6.5 0.0 all-reduce.5.cloned.1.call-start
  6.5 0.8 broadcast_add_fusion
  7.4 0.8 multiply_bitcast_fusion.1
  8.2 1.4 constant_dynamic-slice_fusion.1
  9.6 0.6 iota_compare_fusion.1
  10.3 0.0 copy-done
  10.3 10.8 %convolution_convert_fusion = bf16[1280,2560]{1,0:T(8,128)(2,1)S(1)} fusion(bf16[1280,1280]{1,0:T(8,128)(2,1)S(1)} %bitcast.89, bf16[1280,2560]{1,0:T(8,128)(2,1)} %param.11), kind=kOutput, calls=%fused_computation | convolution fusion | flops 8391884800 | bytes 16384000 | tf_op jit(solution)/shard_map/dot_general | solution.py:70
  21.1 0.0 copy-start.10
  21.1 2.8 %fusion.18 = (bf16[640,1280]{1,0:T(8,128)(2,1)}, bf16[640,1280]{1,0:T(8,128)(2,1)}, bf16[640,1280]{1,0:T(8,128)(2,1)}, bf16[640,1280]{1,0:T(8,128)(2,1)}) fusion(bf16[1280,2560]{1,0:T(8,128)(2,1)S(1)} %convolution_convert_fusion), kind=kLoop, calls=%fused_computation.53 | loop fusion | bytes 13107200 | tf_op jit(solution)/shard_map/slice | solution.py:88
  23.9 3.5 %copy.16 = bf16[640,1280]{0,1:T(8,128)(2,1)} copy(bf16[640,1280]{1,0:T(8,128)(2,1)} %get-tuple-element.26) | data formatting | bytes 3276800 | tf_op jit(solution)/shard_map/slice | solution.py:87
  27.4 0.0 copy-done.10
  27.4 1.4 convolution_convert_fusion.1
  28.9 25.1 %all_gather.3 = bf16[256,1280]{0,1:T(8,128)(2,1)S(1)} all-gather(bf16[256,80]{0,1:T(8,128)(2,1)S(1)} %convolution_convert_fusion.1), channel_id=1, replica_groups=mesh['grp'=2,'seq'=16] {'seq'}, dimensions={1}, use_global_device_ids=true | all-gather | bytes 696320 | tf_op jit(solution)/shard_map/all_gather | solution.py:77
  54.0 0.9 fusion.19
  54.9 0.6 iota_compare_fusion
  55.5 3.5 %copy.17 = bf16[640,1280]{0,1:T(8,128)(2,1)} copy(bf16[640,1280]{1,0:T(8,128)(2,1)} %get-tuple-element.25) | data formatting | bytes 3276800 | tf_op jit(solution)/shard_map/slice | solution.py:87
  59.1 2.7 %fusion.20 = f32[20,128,640]{2,1,0:T(8,128)S(1)} fusion(bf16[128,20,64]{0,2,1:T(8,128)(2,1)} %bitcast.98, bf16[640,20,64]{0,2,1:T(8,128)(2,1)} %bitcast.92), kind=kOutput, calls=%fused_computation.55 | convolution fusion | flops 209715200 | bytes 8519680 | tf_op jit(solution)/shard_map/qhd,jhd->hqj/dot_general | solution.py:23
  61.8 0.0 copy-start.1
  61.8 0.0 copy-start.3
  61.8 0.0 copy-start.9
  61.9 0.0 copy-done.11
  61.9 0.1 broadcast_multiply_fusion.1
  61.9 0.0 copy-done.6
  61.9 0.0 copy-done.7
  61.9 1.6 fusion.2
  63.5 1.0 copy-done.3
  64.5 0.3 copy-done.9
  64.8 4.6 %fusion = (f32[20,128]{1,0:T(8,128)S(1)}, f32[20,128]{1,0:T(8,128)S(1)}, f32[20,128,640]{2,1,0:T(8,128)}) fusion(f32[20,128]{1,0:T(8,128)S(1)} %get-tuple-element.33, pred[640]{0:T(1024)(128)(4,1)S(1)} %iota_compare_fusion.1, f32[20,128]{1,0:T(8,128)S(1)} %get-tuple-element.31, f32[20,128,640]{2,1,0:T(8,128)S(1)} %fusion.20, ...), kind=kOutput, calls=%fused_computation.10 | convolution fusion | flops 222817280 | bytes 15114880 | tf_op jit(solution)/shard_map/qhd,jhd->hqj/dot_general | solution.py:23
  69.4 2.0 convert_reduce_fusion
  71.4 3.5 %copy.15 = bf16[640,1280]{0,1:T(8,128)(2,1)} copy(bf16[640,1280]{1,0:T(8,128)(2,1)} %get-tuple-element.23) | data formatting | bytes 3276800 | tf_op jit(solution)/shard_map/slice | solution.py:88
  74.9 3.5 %copy.18 = bf16[640,1280]{0,1:T(8,128)(2,1)} copy(bf16[640,1280]{1,0:T(8,128)(2,1)} %get-tuple-element.24) | data formatting | bytes 3276800 | tf_op jit(solution)/shard_map/slice | solution.py:88
  78.4 7.1 %convert_reduce_fusion.2 = (f32[20,128]{1,0:T(8,128)S(1)}, f32[20,128]{1,0:T(8,128)S(1)}) fusion(f32[20,128]{1,0:T(8,128)S(1)} %get-tuple-element.7, f32[20,128]{1,0:T(8,128)S(1)} %get-tuple-element.33, f32[20,128,640]{2,1,0:T(8,128)} %get-tuple-element.36, pred[640]{0:T(1024)(128)(4,1)S(1)} %iota_compare_fusion.1, f32[20,128]{1,0:T(8,128)S(1)} %get-tuple-element.8, ...), kind=kLoop, calls=%fused_computation.7 | loop fusion | flops 22932480 | bytes 13169280 | tf_op jit(solution)/shard_map/reduce_sum | solution.py:35
  85.5 57.8 %all-reduce.2 = (f32[128,20]{0,1:T(8,128)S(1)}, f32[128,20]{0,1:T(8,128)S(1)}) all-reduce(f32[128,20]{0,1:T(8,128)S(1)} %bitcast_maximum_fusion, f32[128,20]{0,1:T(8,128)S(1)} %bitcast.104), channel_id=1, replica_groups=mesh['grp'=2,'seq'=16] {'seq'}, use_global_device_ids=true, to_apply=%region_7.8 | all-reduce | flops 5120 | bytes 40960 | tf_op jit(solution)/shard_map/pmax | solution.py:98
  143.4 6.2 %fusion.3 = f32[128,20,64]{0,2,1:T(8,128)} fusion(bf16[640,20,64]{0,2,1:T(8,128)(2,1)} %bitcast.94, f32[128,20]{0,1:T(8,128)S(1)} %get-tuple-element.38, f32[20,128,640]{2,1,0:T(8,128)} %get-tuple-element.36, f32[20,128]{1,0:T(8,128)S(1)} %get-tuple-element.7, f32[20,128]{1,0:T(8,128)S(1)} %get-tuple-element.33, pred[640]{0:T(1024)(128)(4,1)S(1)} %iota_compare_fusion.1), kind=kOutput, calls=%fused_computation.16 | convolution fusion | flops 218071040 | bytes 8878720 | tf_op jit(solution)/shard_map/hqj,jhd->qhd/dot_general | solution.py:37
  149.6 4.3 %fusion.7 = f32[128,20,64]{0,2,1:T(8,128)S(1)} fusion(bf16[640,20,64]{0,2,1:T(8,128)(2,1)S(1)} %bitcast.96, f32[128,20]{0,1:T(8,128)S(1)} %get-tuple-element.20, f32[20,128,640]{2,1,0:T(8,128)} %copy-done.2, f32[20,128]{1,0:T(8,128)S(1)} %get-tuple-element.34, f32[20,128]{1,0:T(8,128)S(1)} %get-tuple-element.32, pred[640]{0:T(1024)(128)(4,1)S(1)} %iota_compare_fusion), kind=kOutput, calls=%fused_computation.20 | convolution fusion | flops 218071040 | bytes 8878720 | tf_op jit(solution)/shard_map/hqj,jhd->qhd/dot_general | solution.py:37
  153.9 0.3 copy-done.4
  154.2 0.7 slice-done.1
  154.9 2.9 %fusion.6 = f32[128,20,64]{0,2,1:T(8,128)} fusion(f32[128,20,64]{0,2,1:T(8,128)S(1)} %fusion.7, bf16[640,20,64]{0,2,1:T(8,128)(2,1)S(1)} %bitcast.95, f32[128,20]{0,1:T(8,128)S(1)} %get-tuple-element.19, f32[128,20]{0,1:T(8,128)S(1)} %get-tuple-element.18, f32[20,128,640]{2,1,0:T(8,128)S(1)} %bitcast.91, f32[20,128]{1,0:T(8,128)S(1)} %get-tuple-element.8, ...), kind=kOutput, calls=%fused_computation.19 | convolution fusion | flops 218398720 | bytes 9544320 | tf_op jit(solution)/shard_map/hqj,jhd->qhd/dot_general | solution.py:37
  157.9 0.0 all-reduce.5.cloned.1.call-update
  157.9 58.0 %all-reduce = (f32[128,20]{0,1:T(8,128)S(1)}, f32[128,20]{0,1:T(8,128)S(1)}) all-reduce(f32[128,20]{0,1:T(8,128)S(1)} %get-tuple-element.17, f32[128,20]{0,1:T(8,128)S(1)} %get-tuple-element.37), channel_id=1, replica_groups=mesh['grp'=2,'seq'=16] {'seq'}, use_global_device_ids=true, to_apply=%region_11.12 | all-reduce | flops 5120 | bytes 40960 | tf_op jit(solution)/shard_map/psum | solution.py:100
  215.9 33.8 %all-reduce.5.cloned.1.call-done = (f32[128,1280]{0,1:T(8,128)}, f32[128,1280]{0,1:T(8,128)}) async-done(((f32[128,1280]{0,1:T(8,128)}, f32[128,1280]{0,1:T(8,128)}), (f32[128,1280]{0,1:T(8,128)}, f32[128,1280]{0,1:T(8,128)})) %all-reduce.5.cloned.1.call-update) | async-done | bytes 1310736 | tf_op jit(solution)/shard_map/psum | solution.py:100
  249.7 1.1 fusion.11
  250.8 0.0 copy-done.8
  250.8 0.2 fusion.8
  251.0 1.1 fusion.10
  252.2 0.2 fusion.9
  252.4 0.6 pad_maximum_fusion
  (16 shorter events, 0.0 us)
Async XLA Ops:
  6.5 3.7 %copy-start = (bf16[2,640,1280]{2,1,0:T(8,128)(2,1)S(1)}, bf16[2,640,1280]{2,1,0:T(8,128)(2,1)}, u32[]{:S(2)}) copy-start(bf16[2,640,1280]{2,1,0:T(8,128)(2,1)} %param.8) | copy-start | bytes 9830404
  6.5 243.1 %all-reduce.5.cloned.1.call-start = ((), (), s32[]{:S(2)}) async-start(), calls=%async_computation | async-start | bytes 2621440 | tf_op jit(solution)/shard_map/psum | solution.py:100
  21.1 6.3 %copy-start.10 = (bf16[1280,80]{0,1:T(8,128)(2,1)S(1)}, bf16[1280,80]{0,1:T(8,128)(2,1)}, u32[]{:S(2)}) copy-start(bf16[1280,80]{0,1:T(8,128)(2,1)} %param.10) | copy-start | bytes 614404
  54.0 7.9 %copy-start.11 = (f32[20]{0:T(128)S(1)}, f32[20]{0:T(128)}, u32[]{:S(2)}) copy-start(f32[20]{0:T(128)} %param.13) | copy-start | bytes 244
  59.1 2.9 %copy-start.6 = (bf16[640,1280]{0,1:T(8,128)(2,1)S(1)}, bf16[640,1280]{0,1:T(8,128)(2,1)}, u32[]{:S(2)}) copy-start(bf16[640,1280]{0,1:T(8,128)(2,1)} %copy.17) | copy-start | bytes 4915204
  59.1 2.9 %copy-start.7 = (bf16[128,1280]{0,1:T(8,128)(2,1)S(1)}, bf16[128,1280]{0,1:T(8,128)(2,1)}, u32[]{:S(2)}) copy-start(bf16[128,1280]{0,1:T(8,128)(2,1)} %get-tuple-element.28) | copy-start | bytes 983044
  61.8 7.5 %copy-start.1 = (f32[20,128,640]{2,1,0:T(8,128)}, f32[20,128,640]{2,1,0:T(8,128)S(1)}, u32[]{:S(2)}) copy-start(f32[20,128,640]{2,1,0:T(8,128)S(1)} %fusion.20) | copy-start | bytes 19660804
  61.8 2.6 %copy-start.3 = (bf16[640,1280]{0,1:T(8,128)(2,1)S(1)}, bf16[640,1280]{0,1:T(8,128)(2,1)}, u32[]{:S(2)}) copy-start(bf16[640,1280]{0,1:T(8,128)(2,1)} %copy.16) | copy-start | bytes 4915204
  61.8 2.9 %copy-start.9 = (bf16[128,1280]{0,1:T(8,128)(2,1)S(1)}, bf16[128,1280]{0,1:T(8,128)(2,1)}, u32[]{:S(2)}) copy-start(bf16[128,1280]{0,1:T(8,128)(2,1)} %get-tuple-element.27) | copy-start | bytes 983044
  63.5 5.9 %copy-start.2 = (f32[20,128,640]{2,1,0:T(8,128)}, f32[20,128,640]{2,1,0:T(8,128)S(1)}, u32[]{:S(2)}) copy-start(f32[20,128,640]{2,1,0:T(8,128)S(1)} %get-tuple-element.35) | copy-start | bytes 19660804
  143.3 6.3 %copy-start.5 = (bf16[640,1280]{0,1:T(8,128)(2,1)S(1)}, bf16[640,1280]{0,1:T(8,128)(2,1)}, u32[]{:S(2)}) copy-start(bf16[640,1280]{0,1:T(8,128)(2,1)} %copy.18) | copy-start | bytes 4915204
  149.6 4.3 %slice-start = ((s8[6553600]{0:T(1024)(128)(4,1)}), s8[4194304]{0:T(1024)(128)(4,1)S(1)}, s32[]{:S(2)}) async-start(s8[6553600]{0:T(1024)(128)(4,1)} %bitcast.90), calls=%async_computation.1 | async-start | bytes 8388608
  149.6 4.6 %copy-start.4 = (bf16[640,1280]{0,1:T(8,128)(2,1)S(1)}, bf16[640,1280]{0,1:T(8,128)(2,1)}, u32[]{:S(2)}) copy-start(bf16[640,1280]{0,1:T(8,128)(2,1)} %copy.15) | copy-start | bytes 4915204
  149.6 5.3 %slice-start.1 = ((s8[6553600]{0:T(1024)(128)(4,1)}), s8[2359296]{0:T(1024)(128)(4,1)S(1)}, s32[]{:S(2)}) async-start(s8[6553600]{0:T(1024)(128)(4,1)} %bitcast.90), calls=%async_computation.2 | async-start | bytes 4718592
  154.9 95.9 %copy-start.8 = (bf16[1280,80]{0,1:T(8,128)(2,1)S(1)}, bf16[1280,80]{0,1:T(8,128)(2,1)}, u32[]{:S(2)}) copy-start(bf16[1280,80]{0,1:T(8,128)(2,1)} %param.12) | copy-start | bytes 614404
Sparse Core Ops, SparseCore 0:
  158.0 91.5 all-reduce.4
where the time goes:
time: 260 us
  blocking collectives  141 us (54%)
  matrix products  35 us (13%)
  waiting for transfers between devices  33.8 us (13%)
  local copies, waits for them, and re-layouts  21.6 us (8%)
  other arithmetic  15.1 us (6%)
  between operations  13.6 us (5%)
    psum x1, blocking collectives, local(): lax.psum((row_total * factors, rescale(row_context, factors, head_count))...  58 us
    pmax x1, blocking collectives, local(): row_top = lax.pmax(row_peak, 'seq')  57.8 us
    psum x1, waiting for transfers between devices, local(): lax.psum((row_total * factors, rescale(row_context, factors, head_count))...  33.8 us
    all_gather x1, blocking collectives, local(): queries = lax.all_gather(local_query, 'seq', axis=1, tiled=True)  25.1 us
    dot_general x3, matrix products, block_partial(): jnp.einsum('hqj,jhd->qhd', weights, values_split, preferred_element_type=...  13.5 us
    dot_general x1, matrix products, local(): jnp.dot(frame_rows, w_keyval, preferred_element_type=jnp.float32)  10.8 us
    slice x3, local copies, waits for them, and re-layouts, local(): block_values[older_step]  9.87 us
    reduce_sum x2, other arithmetic, block_partial(): row_total = jnp.sum(weights.astype(jnp.float32), axis=2)  9.08 us
  transfers between devices with their start and end apart: 1, of which 1 were waited for; matrix products, arithmetic and copies ran while one was open for 0% of the time, Pallas kernels for 0%

commit v1 on v0

--- a/solution.py
+++ b/solution.py
@@ -4,6 +4,15 @@
 import jax.numpy as jnp
 from jax import lax
 from jax.sharding import PartitionSpec as P
+
+
+def state_pools(vector, net_axis):
+    return jnp.concatenate(
+        jax.lax.all_to_all(
+            jnp.stack([vector for _ in range(jax.lax.axis_size(net_axis))]), net_axis, 0, 0
+        ),
+        1,
+    )
 
 
 def block_partial(
@@ -74,7 +83,7 @@
     local_query = jnp.dot(dec_rows, w_query, preferred_element_type=jnp.float32).astype(
         jnp.bfloat16
     )
-    queries = lax.all_gather(local_query, "seq", axis=1, tiled=True)
+    queries = state_pools(local_query, "seq")
     queries = queries.reshape(step_count, query_rows, head_count, head_size)
     combine = functools.partial(combine_parts, head_count)
     slot_place = (own_index + 1) % devices

time: 260 us -> 241 us (0.927)
  blocking collectives: 141 us -> 120 us
  starting transfers between devices: 0.01 us -> 7.47 us
  other arithmetic: 15.1 us -> 10.5 us
    all_gather x1 -> x0, blocking collectives: 25.1 us -> none  [local(): queries = lax.all_gather(local_query, 'seq', axis=1, tiled=True)]
    all_to_all x0 -> x1, starting transfers between devices: none -> 7.43 us  [state_pools(): jax.lax.all_to_all(jnp.stack([vector for _ in range(jax.lax.axis_size(net...]
    pmax x1, blocking collectives: 57.8 us -> 61.8 us  [local(): row_top = lax.pmax(row_peak, 'seq')]
    reduce_sum x2, other arithmetic: 9.08 us -> 6.28 us  [block_partial(): row_total = jnp.sum(weights.astype(jnp.float32), axis=2)]
  transfers between devices with their start and end apart: 1 -> 2, of which waited for: 1 -> 1; matrix products, arithmetic and copies ran while one was open for 0% -> 12% of each run, Pallas kernels for 0% -> 0%
where the time goes in v1:
time: 241 us; the launch traced here: 240 us
  blocking collectives  120 us (50%)
  waiting for transfers between devices  33.8 us (14%)
  matrix products  33.3 us (14%)
  local copies, waits for them, and re-layouts  21.8 us (9%)
  between operations  13.6 us (6%)
  other arithmetic  10.5 us (4%)
  starting transfers between devices  7.47 us (3%)
    pmax x1, blocking collectives, local(): row_top = lax.pmax(row_peak, 'seq')  61.8 us
    psum x1, blocking collectives, local(): lax.psum((row_total * factors, rescale(row_context, factors, head_count))...  58 us
    psum x1, waiting for transfers between devices, local(): lax.psum((row_total * factors, rescale(row_context, factors, head_count))...  33.8 us
    dot_general x3, matrix products, block_partial(): jnp.einsum('hqj,jhd->qhd', weights, values_split, preferred_element_type=...  13.5 us
    dot_general x1, matrix products, local(): jnp.dot(frame_rows, w_keyval, preferred_element_type=jnp.float32)  10.8 us
    slice x3, local copies, waits for them, and re-layouts, local(): block_values[older_step]  9.86 us
    all_to_all x1, starting transfers between devices, state_pools(): jax.lax.all_to_all(jnp.stack([vector for _ in range(jax.lax.axis_size(net...  7.43 us
    slice x2, local copies, waits for them, and re-layouts, local(): block_keys[older_step]  7.1 us
  transfers between devices with their start and end apart: 2, of which 1 were waited for; matrix products, arithmetic and copies ran while one was open for 12% of the time, Pallas kernels for 0%

profile of v1, /device:TPU:0, one launch (start us, length us, event | category | flops | bytes accessed | tf_op | source)
XLA Modules:
  0.0 240.2 jit_solution(14695571678892669176)
XLA Ops:
  6.5 0.0 copy-start
  6.5 1.6 convolution_convert_fusion.1
  8.2 0.9 stack.8
  9.1 7.4 %all-to-all-start = ((bf16[16,256,80]{1,2,0:T(8,128)(2,1)}), bf16[16,256,80]{1,2,0:T(8,128)(2,1)}, u32[]{:S(2)}, u32[]{:S(2)}) async-start(bf16[16,256,80]{1,2,0:T(8,128)(2,1)} %stack.8), calls=%async_computation | async-start | bytes 1310720 | tf_op jit(solution)/shard_map/all_to_all | solution.py:11
  16.5 0.0 all-reduce.5.cloned.1.call-start
  16.5 0.0 copy-done
  16.5 10.8 %convolution_convert_fusion = bf16[1280,2560]{1,0:T(8,128)(2,1)S(1)} fusion(bf16[1280,1280]{1,0:T(8,128)(2,1)S(1)} %bitcast.90, bf16[1280,2560]{1,0:T(8,128)(2,1)} %param.11), kind=kOutput, calls=%fused_computation | convolution fusion | flops 8391884800 | bytes 16384000 | tf_op jit(solution)/shard_map/dot_general | solution.py:79
  27.4 2.8 %fusion.18 = (bf16[640,1280]{1,0:T(8,128)(2,1)}, bf16[640,1280]{1,0:T(8,128)(2,1)}, bf16[640,1280]{1,0:T(8,128)(2,1)}, bf16[640,1280]{1,0:T(8,128)(2,1)}) fusion(bf16[1280,2560]{1,0:T(8,128)(2,1)S(1)} %convolution_convert_fusion), kind=kLoop, calls=%fused_computation.53 | loop fusion | bytes 13107200 | tf_op jit(solution)/shard_map/slice | solution.py:97
  30.2 3.6 %copy.16 = bf16[640,1280]{0,1:T(8,128)(2,1)} copy(bf16[640,1280]{1,0:T(8,128)(2,1)} %get-tuple-element.26) | data formatting | bytes 3276800 | tf_op jit(solution)/shard_map/slice | solution.py:96
  33.7 3.5 %copy.17 = bf16[640,1280]{0,1:T(8,128)(2,1)} copy(bf16[640,1280]{1,0:T(8,128)(2,1)} %get-tuple-element.25) | data formatting | bytes 3276800 | tf_op jit(solution)/shard_map/slice | solution.py:96
  37.3 3.5 %copy.15 = bf16[640,1280]{0,1:T(8,128)(2,1)} copy(bf16[640,1280]{1,0:T(8,128)(2,1)} %get-tuple-element.23) | data formatting | bytes 3276800 | tf_op jit(solution)/shard_map/slice | solution.py:97
  40.8 3.5 %copy.18 = bf16[640,1280]{0,1:T(8,128)(2,1)} copy(bf16[640,1280]{1,0:T(8,128)(2,1)} %get-tuple-element.24) | data formatting | bytes 3276800 | tf_op jit(solution)/shard_map/slice | solution.py:97
  44.3 0.0 copy-done.9
  44.3 0.6 constant_dynamic-slice_fusion.1
  44.9 0.6 iota_compare_fusion.1
  45.6 0.6 iota_compare_fusion
  46.1 0.0 copy-done.11
  46.2 0.0 copy-done.10
  46.2 0.1 broadcast_multiply_fusion.1
  46.3 0.0 all-to-all-done
  46.3 1.2 fusion.19
  47.5 2.5 %fusion.20 = f32[20,128,640]{2,1,0:T(8,128)S(1)} fusion(bf16[128,20,64]{0,2,1:T(8,128)(2,1)S(1)} %bitcast.99, bf16[640,20,64]{0,2,1:T(8,128)(2,1)} %bitcast.93), kind=kOutput, calls=%fused_computation.55 | convolution fusion | flops 209715200 | bytes 8519680 | tf_op jit(solution)/shard_map/qhd,jhd->hqj/dot_general | solution.py:32
  50.0 0.0 copy-start.1
  50.0 0.0 copy-start.4
  50.0 0.0 copy-done.7
  50.0 1.6 fusion.2
  51.6 1.0 copy-done.4
  52.6 2.9 %fusion = (f32[20,128]{1,0:T(8,128)S(1)}, f32[20,128]{1,0:T(8,128)S(1)}, f32[20,128,640]{2,1,0:T(8,128)S(1)}) fusion(f32[20,128]{1,0:T(8,128)S(1)} %get-tuple-element.33, pred[640]{0:T(1024)(128)(4,1)S(1)} %iota_compare_fusion.1, f32[20,128]{1,0:T(8,128)S(1)} %get-tuple-element.31, f32[20,128,640]{2,1,0:T(8,128)S(1)} %fusion.20, ...), kind=kOutput, calls=%fused_computation.10 | convolution fusion | flops 222817280 | bytes 15114880 | tf_op jit(solution)/shard_map/qhd,jhd->hqj/dot_general | solution.py:32
  55.6 0.0 copy-done.2
  55.6 2.0 convert_reduce_fusion
  57.6 0.0 copy-done.1
  57.6 4.3 %convert_reduce_fusion.2 = (f32[20,128]{1,0:T(8,128)S(1)}, f32[20,128]{1,0:T(8,128)S(1)}) fusion(f32[20,128]{1,0:T(8,128)S(1)} %get-tuple-element.7, f32[20,128]{1,0:T(8,128)S(1)} %get-tuple-element.33, f32[20,128,640]{2,1,0:T(8,128)S(1)} %get-tuple-element.36, pred[640]{0:T(1024)(128)(4,1)S(1)} %iota_compare_fusion.1, f32[20,128]{1,0:T(8,128)S(1)} %get-tuple-element.8, ...), kind=kLoop, calls=%fused_computation.7 | loop fusion | flops 22932480 | bytes 13169280 | tf_op jit(solution)/shard_map/reduce_sum | solution.py:44
  61.9 0.0 copy-done.3
  61.9 61.8 %all-reduce.2 = (f32[128,20]{0,1:T(8,128)S(1)}, f32[128,20]{0,1:T(8,128)S(1)}) all-reduce(f32[128,20]{0,1:T(8,128)S(1)} %bitcast_maximum_fusion, f32[128,20]{0,1:T(8,128)S(1)} %bitcast.105), channel_id=1, replica_groups=mesh['grp'=2,'seq'=16] {'seq'}, use_global_device_ids=true, to_apply=%region_7.8 | all-reduce | flops 5120 | bytes 40960 | tf_op jit(solution)/shard_map/pmax | solution.py:107
  123.7 6.2 %fusion.3 = f32[128,20,64]{0,2,1:T(8,128)} fusion(bf16[640,20,64]{0,2,1:T(8,128)(2,1)} %bitcast.95, f32[128,20]{0,1:T(8,128)S(1)} %get-tuple-element.38, f32[20,128,640]{2,1,0:T(8,128)} %copy-done.3, f32[20,128]{1,0:T(8,128)S(1)} %get-tuple-element.7, f32[20,128]{1,0:T(8,128)S(1)} %get-tuple-element.33, pred[640]{0:T(1024)(128)(4,1)S(1)} %iota_compare_fusion.1), kind=kOutput, calls=%fused_computation.16 | convolution fusion | flops 218071040 | bytes 8878720 | tf_op jit(solution)/shard_map/hqj,jhd->qhd/dot_general | solution.py:46
  130.0 4.3 %fusion.7 = f32[128,20,64]{0,2,1:T(8,128)S(1)} fusion(bf16[640,20,64]{0,2,1:T(8,128)(2,1)S(1)} %bitcast.97, f32[128,20]{0,1:T(8,128)S(1)} %get-tuple-element.20, f32[20,128,640]{2,1,0:T(8,128)} %copy-done.2, f32[20,128]{1,0:T(8,128)S(1)} %get-tuple-element.34, f32[20,128]{1,0:T(8,128)S(1)} %get-tuple-element.32, pred[640]{0:T(1024)(128)(4,1)S(1)} %iota_compare_fusion), kind=kOutput, calls=%fused_computation.20 | convolution fusion | flops 218071040 | bytes 8878720 | tf_op jit(solution)/shard_map/hqj,jhd->qhd/dot_general | solution.py:46
  134.3 0.3 copy-done.5
  134.6 0.7 slice-done.1
  135.3 3.0 %fusion.6 = f32[128,20,64]{0,2,1:T(8,128)} fusion(f32[128,20,64]{0,2,1:T(8,128)S(1)} %fusion.7, bf16[640,20,64]{0,2,1:T(8,128)(2,1)S(1)} %bitcast.96, f32[128,20]{0,1:T(8,128)S(1)} %get-tuple-element.19, f32[128,20]{0,1:T(8,128)S(1)} %get-tuple-element.18, f32[20,128,640]{2,1,0:T(8,128)S(1)} %bitcast.92, f32[20,128]{1,0:T(8,128)S(1)} %get-tuple-element.8, ...), kind=kOutput, calls=%fused_computation.19 | convolution fusion | flops 218398720 | bytes 9544320 | tf_op jit(solution)/shard_map/hqj,jhd->qhd/dot_general | solution.py:46
  138.3 0.0 all-reduce.5.cloned.1.call-update
  138.3 58.0 %all-reduce = (f32[128,20]{0,1:T(8,128)S(1)}, f32[128,20]{0,1:T(8,128)S(1)}) all-reduce(f32[128,20]{0,1:T(8,128)S(1)} %get-tuple-element.17, f32[128,20]{0,1:T(8,128)S(1)} %get-tuple-element.37), channel_id=1, replica_groups=mesh['grp'=2,'seq'=16] {'seq'}, use_global_device_ids=true, to_apply=%region_11.12 | all-reduce | flops 5120 | bytes 40960 | tf_op jit(solution)/shard_map/psum | solution.py:109
  196.3 33.8 %all-reduce.5.cloned.1.call-done = (f32[128,1280]{0,1:T(8,128)}, f32[128,1280]{0,1:T(8,128)}) async-done(((f32[128,1280]{0,1:T(8,128)}, f32[128,1280]{0,1:T(8,128)}), (f32[128,1280]{0,1:T(8,128)}, f32[128,1280]{0,1:T(8,128)})) %all-reduce.5.cloned.1.call-update) | async-done | bytes 1310736 | tf_op jit(solution)/shard_map/psum | solution.py:109
  230.0 1.1 fusion.11
  231.2 0.0 copy-done.8
  231.2 0.2 fusion.8
  231.4 1.1 fusion.10
  232.5 0.2 fusion.9
  232.8 0.6 pad_maximum_fusion
  (18 shorter events, 0.1 us)
Async XLA Ops:
  6.5 10.0 %copy-start = (bf16[2,640,1280]{2,1,0:T(8,128)(2,1)S(1)}, bf16[2,640,1280]{2,1,0:T(8,128)(2,1)}, u32[]{:S(2)}) copy-start(bf16[2,640,1280]{2,1,0:T(8,128)(2,1)} %param.8) | copy-start | bytes 9830404
  9.1 37.2 %all-to-all-start = ((bf16[16,256,80]{1,2,0:T(8,128)(2,1)}), bf16[16,256,80]{1,2,0:T(8,128)(2,1)}, u32[]{:S(2)}, u32[]{:S(2)}) async-start(bf16[16,256,80]{1,2,0:T(8,128)(2,1)} %stack.8), calls=%async_computation | async-start | bytes 1310720 | tf_op jit(solution)/shard_map/all_to_all | solution.py:11
  16.5 213.5 %all-reduce.5.cloned.1.call-start = ((), (), s32[]{:S(2)}) async-start(), calls=%async_computation.1 | async-start | bytes 2621440 | tf_op jit(solution)/shard_map/psum | solution.py:109
  30.2 14.1 %copy-start.9 = (s32[2,16]{1,0:T(2,128)S(1)}, s32[2,16]{1,0:T(2,128)}, u32[]{:S(2)}) copy-start(s32[2,16]{1,0:T(2,128)} %param.14) | copy-start | bytes 388
  30.2 15.9 %copy-start.11 = (s32[2,128]{1,0:T(2,128)S(1)}, s32[2,128]{1,0:T(2,128)}, u32[]{:S(2)}) copy-start(s32[2,128]{1,0:T(2,128)} %param.15) | copy-start | bytes 3076
  30.2 16.0 %copy-start.10 = (f32[20]{0:T(128)S(1)}, f32[20]{0:T(128)}, u32[]{:S(2)}) copy-start(f32[20]{0:T(128)} %param.13) | copy-start | bytes 244
  46.3 3.8 %copy-start.7 = (bf16[640,1280]{0,1:T(8,128)(2,1)S(1)}, bf16[640,1280]{0,1:T(8,128)(2,1)}, u32[]{:S(2)}) copy-start(bf16[640,1280]{0,1:T(8,128)(2,1)} %copy.17) | copy-start | bytes 4915204
  50.0 7.6 %copy-start.1 = (f32[20,128,640]{2,1,0:T(8,128)}, f32[20,128,640]{2,1,0:T(8,128)S(1)}, u32[]{:S(2)}) copy-start(f32[20,128,640]{2,1,0:T(8,128)S(1)} %fusion.20) | copy-start | bytes 19660804
  50.0 2.6 %copy-start.4 = (bf16[640,1280]{0,1:T(8,128)(2,1)S(1)}, bf16[640,1280]{0,1:T(8,128)(2,1)}, u32[]{:S(2)}) copy-start(bf16[640,1280]{0,1:T(8,128)(2,1)} %copy.16) | copy-start | bytes 4915204
  51.6 3.9 %copy-start.2 = (f32[20,128,640]{2,1,0:T(8,128)}, f32[20,128,640]{2,1,0:T(8,128)S(1)}, u32[]{:S(2)}) copy-start(f32[20,128,640]{2,1,0:T(8,128)S(1)} %get-tuple-element.35) | copy-start | bytes 19660804
  55.5 6.3 %copy-start.3 = (f32[20,128,640]{2,1,0:T(8,128)}, f32[20,128,640]{2,1,0:T(8,128)S(1)}, u32[]{:S(2)}) copy-start(f32[20,128,640]{2,1,0:T(8,128)S(1)} %get-tuple-element.36) | copy-start | bytes 19660804
  123.7 6.3 %copy-start.6 = (bf16[640,1280]{0,1:T(8,128)(2,1)S(1)}, bf16[640,1280]{0,1:T(8,128)(2,1)}, u32[]{:S(2)}) copy-start(bf16[640,1280]{0,1:T(8,128)(2,1)} %copy.18) | copy-start | bytes 4915204
  130.0 4.3 %slice-start = ((s8[6553600]{0:T(1024)(128)(4,1)}), s8[4194304]{0:T(1024)(128)(4,1)S(1)}, s32[]{:S(2)}) async-start(s8[6553600]{0:T(1024)(128)(4,1)} %bitcast.91), calls=%async_computation.2 | async-start | bytes 8388608
  130.0 4.6 %copy-start.5 = (bf16[640,1280]{0,1:T(8,128)(2,1)S(1)}, bf16[640,1280]{0,1:T(8,128)(2,1)}, u32[]{:S(2)}) copy-start(bf16[640,1280]{0,1:T(8,128)(2,1)} %copy.15) | copy-start | bytes 4915204
  130.0 5.3 %slice-start.1 = ((s8[6553600]{0:T(1024)(128)(4,1)}), s8[2359296]{0:T(1024)(128)(4,1)S(1)}, s32[]{:S(2)}) async-start(s8[6553600]{0:T(1024)(128)(4,1)} %bitcast.91), calls=%async_computation.3 | async-start | bytes 4718592
  135.3 95.9 %copy-start.8 = (bf16[1280,80]{0,1:T(8,128)(2,1)S(1)}, bf16[1280,80]{0,1:T(8,128)(2,1)}, u32[]{:S(2)}) copy-start(bf16[1280,80]{0,1:T(8,128)(2,1)} %param.12) | copy-start | bytes 614404
Sparse Core Ops, SparseCore 0:
  138.4 91.5 all-reduce.4
